TPU v7x, 256 devices: a whole 4x4x8 slice. The times are simulated.
256 devices in a mesh: gx: 4 (over y_lo, core), gz: 8 (over y_hi, x), ta: 8 (over z).
Axes of the slice: x: 4, y: 4 (y_hi: 2, y_lo: 2; y = y_hi * 2 + y_lo), z: 8, core: 2. Of those that a mesh axis runs over, the one named last changes fastest.
Arguments:
- links: float32 [4, 2, 3, 3, 32, 32, 512], P(None, None, None, None, 'ta', 'gz', 'gx'), may hold values from -1 to 1, as said below
Outputs:
- force: float32 [4, 2, 3, 3, 32, 32, 512], P(None, None, None, None, 'ta', 'gz', 'gx')
Inputs may be any that keep to these rules, and one draw needn't show every extreme that they name: Every link matrix (real part links[mu, 0], imaginary part links[mu, 1]) is special unitary, up to float32 rounding.
All inputs are finite; a program needn't handle non-finite values.
Results may differ from a plain program's by a relative error of at most 0.0003.
Values sent between devices are 32-bit elements; how exact they have to be, the bound alone decides.
A program may use at most 64 MiB of HBM per device.

v0:
```python
import jax
import jax.numpy as jnp
from jax import lax
from jax.sharding import PartitionSpec as P

NX = 16


COEFF = -1.9


def padded(block, sides, width):
    for axis, dim in sides:
        count = lax.axis_size(axis)
        forward = [(i, i + 1) for i in range(count - 1)]
        forward.append((count - 1, 0))
        backward = [(target, source) for source, target in forward]
        low = lax.ppermute(
            lax.slice_in_dim(block, block.shape[dim] - width, None, axis=dim), axis, forward
        )
        high = lax.ppermute(lax.slice_in_dim(block, 0, width, axis=dim), axis, backward)
        block = jnp.concatenate([low, block, high], axis=dim)
    return block


def matprod(left, right):
    total = left[:, 0][:, None] * right[0][None, :]
    total = total + left[:, 1][:, None] * right[1][None, :]
    return total + left[:, 2][:, None] * right[2][None, :]


def complex_mul(left, right):
    return (
        matprod(left[0], right[0]) - matprod(left[1], right[1]),
        matprod(left[0], right[1]) + matprod(left[1], right[0]),
    )


def dagger(matrix):
    return (jnp.swapaxes(matrix[0], 0, 1), -jnp.swapaxes(matrix[1], 0, 1))


def unit_step(direction, sign):
    offset = [0, 0, 0, 0]
    offset[direction] = sign
    return tuple(offset)


def joined(first_step, second_step):
    return tuple((first_step[position] + second_step[position] for position in range(4)))


def gauge_force(fetch_link):
    blocks = []
    still = (0, 0, 0, 0)
    for direction in range(4):
        ahead = unit_step(direction, 1)
        summed = None
        for transverse in range(4):
            if transverse == direction:
                continue
            side_up = unit_step(transverse, 1)
            side_down = unit_step(transverse, -1)
            upper = complex_mul(
                complex_mul(fetch_link(transverse, ahead), dagger(fetch_link(direction, side_up))),
                dagger(fetch_link(transverse, still)),
            )
            lower = complex_mul(
                complex_mul(
                    dagger(fetch_link(transverse, joined(ahead, side_down))),
                    dagger(fetch_link(direction, side_down)),
                ),
                fetch_link(transverse, side_down),
            )
            staple = (upper[0] + lower[0], upper[1] + lower[1])
            summed = staple if summed is None else (summed[0] + staple[0], summed[1] + staple[1])
        loop_matrix = complex_mul(fetch_link(direction, still), summed)
        real_part = 0.5 * (loop_matrix[0] - jnp.swapaxes(loop_matrix[0], 0, 1))
        imag_part = 0.5 * (loop_matrix[1] + jnp.swapaxes(loop_matrix[1], 0, 1))
        trace_third = (loop_matrix[1][0, 0] + loop_matrix[1][1, 1] + loop_matrix[1][2, 2]) / 3.0
        identity = jnp.eye(3, dtype=jnp.float32).reshape((3, 3) + (1,) * trace_third.ndim)
        imag_part = imag_part - identity * trace_third
        blocks.append(COEFF * jnp.stack([real_part, imag_part], axis=0))
    return jnp.stack(blocks, axis=0)


def complete_rows(wider):
    real0 = wider[:, 0, 0]
    imag0 = wider[:, 1, 0]
    real1 = wider[:, 0, 1]
    imag1 = wider[:, 1, 1]
    real_cols = []
    imag_cols = []
    for column in range(3):
        next_col = (column + 1) % 3
        last_col = (column + 2) % 3
        cross_real = (
            real0[:, next_col] * real1[:, last_col]
            - imag0[:, next_col] * imag1[:, last_col]
            - real0[:, last_col] * real1[:, next_col]
            + imag0[:, last_col] * imag1[:, next_col]
        )
        cross_imag = (
            real0[:, next_col] * imag1[:, last_col]
            + imag0[:, next_col] * real1[:, last_col]
            - real0[:, last_col] * imag1[:, next_col]
            - imag0[:, last_col] * real1[:, next_col]
        )
        real_cols.append(cross_real)
        imag_cols.append(-cross_imag)
    third = jnp.stack([jnp.stack(real_cols, axis=1), jnp.stack(imag_cols, axis=1)], axis=1)
    return jnp.concatenate([wider, third[:, :, None]], axis=2)


def per_device(links):
    payload = links[:, :, 0:2]
    wider = padded(payload, (("gx", 6),), NX)
    wider = padded(wider, (("ta", 4), ("gz", 5)), 1)
    wider = complete_rows(wider)
    time_len = links.shape[4]
    depth_len = links.shape[5]
    flat_len = links.shape[6]
    column = lax.broadcasted_iota(jnp.int32, (flat_len,), 0) % NX
    right_edge = column == NX - 1
    left_edge = column == 0

    def fetch_link(direction, offset):
        start = NX + offset[2] * NX
        field = wider[
            direction,
            :,
            :,
            :,
            1 + offset[0] : 1 + offset[0] + time_len,
            1 + offset[1] : 1 + offset[1] + depth_len,
            start : start + flat_len,
        ]
        if offset[3] == 1:
            field = jnp.where(
                right_edge, jnp.roll(field, NX - 1, axis=5), jnp.roll(field, -1, axis=5)
            )
        elif offset[3] == -1:
            field = jnp.where(
                left_edge, jnp.roll(field, 1 - NX, axis=5), jnp.roll(field, 1, axis=5)
            )
        return (field[0], field[1])

    return gauge_force(fetch_link)


def solution(mesh):
    return jax.shard_map(
        per_device,
        mesh=mesh,
        in_specs=(P(None, None, None, None, "ta", "gz", "gx"),),
        out_specs=P(None, None, None, None, "ta", "gz", "gx"),
        check_vma=False,
    )
```

profile of v0, /device:TPU:6, one launch (start us, length us, event | category | flops | bytes accessed | tf_op | source)
XLA Modules:
  0.0 70.1 jit_solution(11727214759005900719)
XLA Ops:
  0.0 1.4 %fusion.22 = (f32[4,2,2,3,4,4,16]{6,5,4,3,2,1,0:T(4,128)S(1)}, f32[4,2,2,3,4,4,16]{6,5,4,3,2,1,0:T(4,128)S(1)}) fusion(f32[4,2,3,3,4,4,128]{6,5,4,3,2,1,0:T(4,128)} %param.1), kind=kLoop, calls=%fused_computation.729 | loop fusion | bytes 196608 | tf_op jit(solution)/shard_map/slice | solution.py:19
  1.7 1.1 %collective-permute-start.1 = (f32[4,2,2,3,4,4,16]{6,0,5,4,3,2,1:T(4,128)S(1)}, f32[4,2,2,3,4,4,16]{6,0,5,4,3,2,1:T(4,128)S(1)}, u32[]{:S(2)}, u32[]{:S(2)}) collective-permute-start(f32[4,2,2,3,4,4,16]{6,0,5,4,3,2,1:T(4,128)S(1)} %copy.21), channel_id=1, source_target_pairs={{64,0},{128,64},{192,128},{0,192},{65,1},{129,65},{193,129},{1,193... | collective-permute-start | bytes 147464 | tf_op jit(solution)/shard_map/ppermute | solution.py:21
  3.4 8.5 %collective-permute-done.1 = f32[4,2,2,3,4,4,16]{6,0,5,4,3,2,1:T(4,128)S(1)} collective-permute-done((f32[4,2,2,3,4,4,16]{6,0,5,4,3,2,1:T(4,128)S(1)}, f32[4,2,2,3,4,4,16]{6,0,5,4,3,2,1:T(4,128)S(1)}, u32[]{:S(2)}, u32[]{:S(2)}) %collective-permute-start.1) | collective-permute-done | bytes 49184 | tf_op jit(solution)/shard_map/ppermute | solution.py:21
  12.0 1.4 %collective-permute-done = f32[4,2,2,3,4,4,16]{6,0,5,4,3,2,1:T(4,128)S(1)} collective-permute-done((f32[4,2,2,3,4,4,16]{6,0,5,4,3,2,1:T(4,128)S(1)}, f32[4,2,2,3,4,4,16]{6,0,5,4,3,2,1:T(4,128)S(1)}, u32[]{:S(2)}, u32[]{:S(2)}) %collective-permute-start) | collective-permute-done | bytes 49184 | tf_op jit(solution)/shard_map/ppermute | solution.py:18
  13.7 2.0 %collective-permute-start.2 = (f32[4,2,2,3,1,4,160]{6,0,5,4,3,2,1:T(4,128)S(1)}, f32[4,2,2,3,1,4,160]{6,0,5,4,3,2,1:T(4,128)S(1)}, u32[]{:S(2)}, u32[]{:S(2)}) collective-permute-start(f32[4,2,2,3,1,4,160]{6,0,5,4,3,2,1:T(4,128)S(1)} %get-tuple-element.90), channel_id=1, source_target_pairs={{0,1},{1,2},{2,3},{3,4},{4,5},{5,6},{6,7},{7,0},{8,9},{9,10},{10,1... | collective-permute-start | bytes 368648 | tf_op jit(solution)/shard_map/ppermute | solution.py:18
  15.7 4.0 %collective-permute-start.3 = (f32[4,2,2,3,1,4,160]{6,0,5,4,3,2,1:T(4,128)S(1)}, f32[4,2,2,3,1,4,160]{6,0,5,4,3,2,1:T(4,128)S(1)}, u32[]{:S(2)}, u32[]{:S(2)}) collective-permute-start(f32[4,2,2,3,1,4,160]{6,0,5,4,3,2,1:T(4,128)S(1)} %get-tuple-element.91), channel_id=1, source_target_pairs={{1,0},{2,1},{3,2},{4,3},{5,4},{6,5},{7,6},{0,7},{9,8},{10,9},{11,1... | collective-permute-start | bytes 368648 | tf_op jit(solution)/shard_map/ppermute | solution.py:21
  19.7 4.1 %collective-permute-done.2 = f32[4,2,2,3,1,4,160]{6,0,5,4,3,2,1:T(4,128)S(1)} collective-permute-done((f32[4,2,2,3,1,4,160]{6,0,5,4,3,2,1:T(4,128)S(1)}, f32[4,2,2,3,1,4,160]{6,0,5,4,3,2,1:T(4,128)S(1)}, u32[]{:S(2)}, u32[]{:S(2)}) %collective-permute-start.2) | collective-permute-done | bytes 122912 | tf_op jit(solution)/shard_map/ppermute | solution.py:18
  24.2 3.0 %collective-permute-start.4 = (f32[4,2,2,3,6,1,160]{6,0,5,4,3,2,1:T(4,128)S(1)}, f32[4,2,2,3,6,1,160]{6,0,5,4,3,2,1:T(4,128)S(1)}, u32[]{:S(2)}, u32[]{:S(2)}) collective-permute-start(f32[4,2,2,3,6,1,160]{6,0,5,4,3,2,1:T(4,128)S(1)} %get-tuple-element.84), channel_id=1, source_target_pairs={{0,8},{8,16},{16,24},{24,32},{32,40},{40,48},{48,56},{56,0},{1,9},... | collective-permute-start | bytes 552968 | tf_op jit(solution)/shard_map/ppermute | solution.py:18
  27.6 4.6 %collective-permute-done.4 = f32[4,2,2,3,6,1,160]{6,0,5,4,3,2,1:T(4,128)S(1)} collective-permute-done((f32[4,2,2,3,6,1,160]{6,0,5,4,3,2,1:T(4,128)S(1)}, f32[4,2,2,3,6,1,160]{6,0,5,4,3,2,1:T(4,128)S(1)}, u32[]{:S(2)}, u32[]{:S(2)}) %collective-permute-start.4) | collective-permute-done | bytes 184352 | tf_op jit(solution)/shard_map/ppermute | solution.py:18
  32.1 5.8 %collective-permute-done.5 = f32[4,2,2,3,6,1,160]{6,0,5,4,3,2,1:T(4,128)S(1)} collective-permute-done((f32[4,2,2,3,6,1,160]{6,0,5,4,3,2,1:T(4,128)S(1)}, f32[4,2,2,3,6,1,160]{6,0,5,4,3,2,1:T(4,128)S(1)}, u32[]{:S(2)}, u32[]{:S(2)}) %collective-permute-start.5) | collective-permute-done | bytes 184352 | tf_op jit(solution)/shard_map/ppermute | solution.py:21
  38.0 1.1 %pad_maximum_fusion.1 = f32[4,2,2,3,6,6,160]{6,0,5,4,3,2,1:T(4,128)S(1)} fusion(f32[4,2,2,3,6,1,160]{6,0,5,4,3,2,1:T(4,128)S(1)} %collective-permute-done.5, f32[4,2,2,3,1,4,160]{6,0,5,4,3,2,1:T(4,128)S(1)} %collective-permute-done.3, f32[4,2,2,3,4,4,16]{6,0,5,4,3,2,1:T(4,128)S(1)} %collective-permute-done.1, f32[4,2,2,3,4,4,128]{6,0,5,4,3,2,1:T(4,128)S(1)} %copy.20, ...), kind=kLoop, calls=%fused_computation.1 | loop fusion | flops 1658880 | bytes 2211840 | tf_op jit(solution)/shard_map/concatenate | solution.py:22
  40.8 1.5 %pad_maximum_fusion = f32[4,2,3,3,6,6,160]{6,0,5,4,3,2,1:T(4,128)S(1)} fusion(f32[4,2,1,3,6,6,160]{6,0,5,4,3,2,1:T(4,128)S(1)} %maximum_bitcast_fusion, f32[4,2,2,3,6,1,160]{6,0,5,4,3,2,1:T(4,128)S(1)} %collective-permute-done.5, f32[4,2,2,3,1,4,160]{6,0,5,4,3,2,1:T(4,128)S(1)} %collective-permute-done.3, ...), kind=kLoop, calls=%fused_computation | loop fusion | flops 2903040 | bytes 3317760 | tf_op jit(solution)/shard_map/concatenate | solution.py:112
  42.3 2.5 %slice_negate_fusion.23 = (f32[1,1,3,3,4,4,128]{6,0,5,4,3,2,1:T(1,128)S(1)}, f32[1,1,3,3,4,4,128]{6,0,5,4,3,2,1:T(1,128)S(1)}, f32[1,1,3,3,4,4,128]{6,0,5,4,3,2,...) fusion(f32[4,2,3,3,6,6,160]{6,0,5,4,3,2,1:T(4,128)S(1)} %pad_ma, ...), kind=kLoop, calls=%fused_computation.85 | loop fusion | flops 55296 | bytes 2654208 | tf_op jit(solution)/shard_map/neg | solution.py:40
  45.0 2.7 %fusion.18 = (f32[1,1,3,3,4,4,128]{6,0,5,4,3,2,1:T(1,128)S(1)}, f32[1,1,3,3,4,4,128]{6,0,5,4,3,2,1:T(1,128)S(1)}, f32[1,1,3,3,4,4,128]{6,0,5,4,3,2,1:T(1,128)S(1...) fusion(f32[4,2,3,3,6,6,160]{6,0,5,4,3,2,1:T(4,128)S(1)} %pad_ma, ...), kind=kLoop, calls=%fused_computation.725 | loop fusion | flops 147456 | bytes 2801664 | tf_op jit(solution)/shard_map/slice | solution.py:146
  47.9 2.5 %fusion.19 = (f32[1,1,3,3,4,4,128]{6,0,5,4,3,2,1:T(1,128)S(1)}, f32[1,1,3,3,4,4,128]{6,0,5,4,3,2,1:T(1,128)S(1)}, f32[1,1,3,3,4,4,128]{6,0,5,4,3,2,1:T(1,128)S(1...) fusion(f32[4,2,3,3,6,6,160]{6,0,5,4,3,2,1:T(4,128)S(1)} %pad_ma, ...), kind=kLoop, calls=%fused_computation.726 | loop fusion | flops 73728 | bytes 2801664 | tf_op jit(solution)/shard_map/slice | solution.py:146
  50.3 2.9 %fusion.20 = (f32[1,2,3,3,4,4,128]{6,0,5,4,3,2,1:T(1,128)S(1)}, f32[1,2,3,3,4,4,128]{6,0,5,4,3,2,1:T(1,128)S(1)}, f32[1,2,3,3,4,4,128]{6,0,5,4,3,2,1:T(1,128)S(1...) fusion(f32[4,2,3,3,6,6,160]{6,0,5,4,3,2,1:T(4,128)S(1)} %pad_ma, ...), kind=kLoop, calls=%fused_computation.727 | loop fusion | bytes 2949120 | tf_op jit(solution)/shard_map/slice | solution.py:129
  57.5 0.7 maximum_select_fusion
  61.3 0.5 maximum_select_fusion.6
  62.1 0.7 maximum_select_fusion.1
  64.3 0.4 add_add_fusion.2
  64.7 0.4 add_add_fusion.1
  65.3 0.4 add_add_fusion.10
  65.7 0.4 add_add_fusion.11
  69.1 0.9 %pad_maximum_fusion.2 = f32[4,2,3,3,4,4,128]{6,5,4,3,2,1,0:T(4,128)} fusion(f32[1,2,3,3,4,4,128]{6,5,4,3,2,1,0:T(4,128)S(1)} %maximum_multiply_fusion.3, f32[1,2,3,3,4,4,128]{6,5,4,3,2,1,0:T(4,128)S(1)} %maximum_multiply_fusion.2, f32[1,2,3,3,4,4,128]{6,5,4,3,2,1,0:T(4,128)S(1)} %maximum_multiply_fusion.1, ...), kind=kLoop, calls=%fused_computation.3 | loop fusion | flops 442368 | bytes 1179648 | tf_op jit(solution)/shard_map/stack | solution.py:84
  (291 shorter events, 14.4 us)
Async XLA Ops:
  0.0 3.1 %slice-start = ((f32[4,2,3,3,4,4,128]{6,5,4,3,2,1,0:T(4,128)}), f32[4,2,2,3,4,4,128]{6,5,4,3,2,1,0:T(4,128)S(1)}, s32[]{:S(2)}) async-start(f32[4,2,3,3,4,4,128]{6,5,4,3,2,1,0:T(4,128)} %param.1), calls=%async_computation | async-start | bytes 786432 | tf_op jit(solution)/shard_map/slice | solution.py:116
  1.7 10.3 %collective-permute-start.1 = (f32[4,2,2,3,4,4,16]{6,0,5,4,3,2,1:T(4,128)S(1)}, f32[4,2,2,3,4,4,16]{6,0,5,4,3,2,1:T(4,128)S(1)}, u32[]{:S(2)}, u32[]{:S(2)}) collective-permute-start(f32[4,2,2,3,4,4,16]{6,0,5,4,3,2,1:T(4,128)S(1)} %copy.21), channel_id=1, source_target_pairs={{64,0},{128,64},{192,128},{0,192},{65,1},{129,65},{193,129},{1,193... | collective-permute-start | bytes 147464 | tf_op jit(solution)/shard_map/ppermute | solution.py:21
  3.1 10.3 %collective-permute-start = (f32[4,2,2,3,4,4,16]{6,0,5,4,3,2,1:T(4,128)S(1)}, f32[4,2,2,3,4,4,16]{6,0,5,4,3,2,1:T(4,128)S(1)}, u32[]{:S(2)}, u32[]{:S(2)}) collective-permute-start(f32[4,2,2,3,4,4,16]{6,0,5,4,3,2,1:T(4,128)S(1)} %copy.19), channel_id=1, source_target_pairs={{0,64},{64,128},{128,192},{192,0},{1,65},{65,129},{129,193},{193,1... | collective-permute-start | bytes 147464 | tf_op jit(solution)/shard_map/ppermute | solution.py:18
  13.7 10.1 %collective-permute-start.2 = (f32[4,2,2,3,1,4,160]{6,0,5,4,3,2,1:T(4,128)S(1)}, f32[4,2,2,3,1,4,160]{6,0,5,4,3,2,1:T(4,128)S(1)}, u32[]{:S(2)}, u32[]{:S(2)}) collective-permute-start(f32[4,2,2,3,1,4,160]{6,0,5,4,3,2,1:T(4,128)S(1)} %get-tuple-element.90), channel_id=1, source_target_pairs={{0,1},{1,2},{2,3},{3,4},{4,5},{5,6},{6,7},{7,0},{8,9},{9,10},{10,1... | collective-permute-start | bytes 368648 | tf_op jit(solution)/shard_map/ppermute | solution.py:18
  15.7 8.1 %collective-permute-start.3 = (f32[4,2,2,3,1,4,160]{6,0,5,4,3,2,1:T(4,128)S(1)}, f32[4,2,2,3,1,4,160]{6,0,5,4,3,2,1:T(4,128)S(1)}, u32[]{:S(2)}, u32[]{:S(2)}) collective-permute-start(f32[4,2,2,3,1,4,160]{6,0,5,4,3,2,1:T(4,128)S(1)} %get-tuple-element.91), channel_id=1, source_target_pairs={{1,0},{2,1},{3,2},{4,3},{5,4},{6,5},{7,6},{0,7},{9,8},{10,9},{11,1... | collective-permute-start | bytes 368648 | tf_op jit(solution)/shard_map/ppermute | solution.py:21
  24.2 8.0 %collective-permute-start.4 = (f32[4,2,2,3,6,1,160]{6,0,5,4,3,2,1:T(4,128)S(1)}, f32[4,2,2,3,6,1,160]{6,0,5,4,3,2,1:T(4,128)S(1)}, u32[]{:S(2)}, u32[]{:S(2)}) collective-permute-start(f32[4,2,2,3,6,1,160]{6,0,5,4,3,2,1:T(4,128)S(1)} %get-tuple-element.84), channel_id=1, source_target_pairs={{0,8},{8,16},{16,24},{24,32},{32,40},{40,48},{48,56},{56,0},{1,9},... | collective-permute-start | bytes 552968 | tf_op jit(solution)/shard_map/ppermute | solution.py:18
  27.2 10.7 %collective-permute-start.5 = (f32[4,2,2,3,6,1,160]{6,0,5,4,3,2,1:T(4,128)S(1)}, f32[4,2,2,3,6,1,160]{6,0,5,4,3,2,1:T(4,128)S(1)}, u32[]{:S(2)}, u32[]{:S(2)}) collective-permute-start(f32[4,2,2,3,6,1,160]{6,0,5,4,3,2,1:T(4,128)S(1)} %get-tuple-element.85), channel_id=1, source_target_pairs={{8,0},{16,8},{24,16},{32,24},{40,32},{48,40},{56,48},{0,56},{9,1},... | collective-permute-start | bytes 552968 | tf_op jit(solution)/shard_map/ppermute | solution.py:21
where the time goes:
time: 70.4 us; the launch traced here: 70.1 us
  waiting for transfers between devices  24.4 us (35%)
  other arithmetic  22.5 us (32%)
  local copies, waits for them, and re-layouts  10.9 us (15%)
  starting transfers between devices  10.2 us (14%)
  between operations  2.05 us (3%)
    ppermute x3, waiting for transfers between devices, padded(): lax.ppermute(lax.slice_in_dim(block, 0, width, axis=dim), axis, backward)  14.4 us
    ppermute x3, waiting for transfers between devices, padded(): lax.ppermute(lax.slice_in_dim(block, block.shape[dim] - width, None, axis...  10 us
    slice x2, other arithmetic, fetch_link(): return (field[0], field[1])  5.21 us
    ppermute x3, starting transfers between devices, padded(): lax.ppermute(lax.slice_in_dim(block, block.shape[dim] - width, None, axis...  5.12 us
    ppermute x3, starting transfers between devices, padded(): lax.ppermute(lax.slice_in_dim(block, 0, width, axis=dim), axis, backward)  5.12 us
    slice x1, local copies, waits for them, and re-layouts, fetch_link(): wider[direction, :, :, :, 1 + offset[0]:1 + offset[0] + time_len, 1 + off...  2.89 us
    neg x17, other arithmetic, dagger(): return (jnp.swapaxes(matrix[0], 0, 1), -jnp.swapaxes(matrix[1], 0, 1))  2.77 us
    slice x10, local copies, waits for them, and re-layouts, fetch_link(): jnp.roll(field, 1, axis=5)  1.66 us
  transfers between devices with their start and end apart: 6, of which 5 were waited for; matrix products, arithmetic and copies ran while one was open for 1% of the time, Pallas kernels for 0%

commit v1 on v0

v1 whole, which is shorter than its diff:
```python
import functools

import jax
import jax.numpy as jnp
from jax import lax
from jax.experimental import pallas as pl
from jax.experimental.pallas import tpu as pltpu
from jax.sharding import PartitionSpec as P

MESH = pl.DeviceIdType.MESH
COEFF = -1.9
NX = 16
ROWS = 16
LANES = 128

STEP = (4, 1, 16, 1)
AXIS = (0, 0, 1, 1)
COUNT = (4, 4, 8, 16)
GROUP = (4, 4, 8)
RING = ("ta", "gz", "gx")
PLANES = ((0, 3), (2, 3), (0, 2), (1, 3), (1, 2), (0, 1))


def comp(mu, part, i, j):
    return ((mu * 2 + part) * 3 + i) * 3 + j


def slot(step_dir, link_dir):
    return step_dir * 3 + (link_dir if link_dir < step_dir else link_dir - 1)


def others(direction):
    return [d for d in range(4) if d != direction]


def position(direction):
    iota = lax.broadcasted_iota(jnp.int32, (ROWS, LANES), AXIS[direction])
    return (iota // STEP[direction]) % COUNT[direction]


def turn(value, direction, steps):
    size = (ROWS, LANES)[AXIS[direction]]
    amount = (steps * STEP[direction]) % size
    if amount == 0:
        return value
    return pltpu.roll(value, amount, axis=AXIS[direction])


def pack(loads, buf, direction, high):
    where = position(direction)
    width = GROUP[direction]
    for first in range(0, len(loads), width):
        packed = None
        for j, load in enumerate(loads[first : first + width]):
            moved = turn(load(), direction, j - (width - 1) if high else j)
            packed = moved if packed is None else jnp.where(where == j, moved, packed)
        buf[first // width] = packed


def unpack(buf, index, direction, high):
    width = GROUP[direction]
    j = index % width
    return turn(buf[index // width], direction, width - 1 - j if high else -j)


def cmul(a, b, conj_a=False, conj_b=False):
    (ar, ai), (br, bi) = a, b
    sa = -1 if conj_a else 1
    sb = -1 if conj_b else 1
    return ([(1, ar * br), (-sa * sb, ai * bi)], [(sb, ar * bi), (sa, ai * br)])


def total(terms):
    terms = sorted(terms, key=lambda term: -term[0])
    result = None
    for sign, value in terms:
        if result is None:
            result = value if sign > 0 else -value
        else:
            result = result + value if sign > 0 else result - value
    return result


def dot3(pairs, conj_a=False, conj_b=False, parts="ri"):
    real, imag = [], []
    for a, b in pairs:
        (ar, ai), (br, bi) = a, b
        sa = -1 if conj_a else 1
        sb = -1 if conj_b else 1
        if "r" in parts:
            real += [(1, ar * br), (-sa * sb, ai * bi)]
        if "i" in parts:
            imag += [(sb, ar * bi), (sa, ai * br)]
    return (total(real) if real else None, total(imag) if imag else None)


OFF = ((0, 1), (0, 2), (1, 2))


def leaf(entry, trace):
    values = []
    for i, j in OFF:
        upper = entry(i, j, "ri")
        lower = entry(j, i, "ri")
        values.append(upper[0] - lower[0])
        values.append(upper[1] + lower[1])
    for i in range(2):
        values.append(entry(i, i, "i")[1] - trace)
    return values


def kernel(links_ref, out_ref, u, shifted, store, leaves, wmat, send1, recv1, send2, recv2,
           in_sem, s1, r1, s2, r2):
    fetch = [
        pltpu.make_async_copy(links_ref.at[pl.ds(mu * 18, 18)], u.at[pl.ds(mu * 18, 18)], in_sem.at[mu])
        for mu in range(4)
    ]
    for copy in fetch:
        copy.start()

    index = [lax.axis_index(name) for name in RING]
    size = [lax.axis_size(name) for name in RING]
    below = [{RING[d]: lax.rem(index[d] + size[d] - 1, size[d])} for d in range(3)]
    above = [{RING[d]: lax.rem(index[d] + 1, size[d])} for d in range(3)]
    barrier = pltpu.get_barrier_semaphore()
    for d in (1, 0, 2):
        pl.semaphore_signal(barrier, inc=1, device_id=below[d], device_id_type=MESH)
        pl.semaphore_signal(barrier, inc=1, device_id=above[d], device_id_type=MESH)
    for copy in fetch:
        copy.wait()

    def link(mu, part, i, j):
        return lambda: u[comp(mu, part, i, j)]

    for d in (1, 0, 2):
        loads = [link(nu, part, i, j) for nu in others(d) for part in range(2) for i in range(2) for j in range(3)]
        pack(loads, send1[d], d, high=False)
    pl.semaphore_wait(barrier, 6)
    down = [
        pltpu.make_async_remote_copy(
            src_ref=send1[d], dst_ref=recv1[d], send_sem=s1.at[d], recv_sem=r1.at[d],
            device_id=below[d], device_id_type=MESH,
        )
        for d in range(3)
    ]
    for d in (1, 0, 2):
        down[d].start()

    def make_w(plane, mu, nu):
        def body(v, carry):
            rows = pl.ds(pl.multiple_of(v * 8, 8), 8)

            def get(ref, base):
                return [[(ref[base + i * 3 + j, rows, :], ref[base + 9 + i * 3 + j, rows, :])
                         for j in range(3)] for i in range(3)]

            a = get(u, mu * 18)
            b = get(u, nu * 18)
            for i in range(3):
                for j in range(3):
                    real, imag = dot3([(b[k][i], a[k][j]) for k in range(3)], conj_a=True)
                    wmat[plane * 18 + i * 3 + j, rows, :] = real
                    wmat[plane * 18 + 9 + i * 3 + j, rows, :] = imag
            return carry

        lax.fori_loop(0, 2, body, 0)

    def shift_x():
        edge = position(3) == NX - 1
        for nu in others(3):
            base = slot(3, nu) * 18
            for c in range(18):
                value = u[nu * 18 + c]
                shifted[base + c] = jnp.where(
                    edge, pltpu.roll(value, NX - 1, axis=1), pltpu.roll(value, LANES - 1, axis=1)
                )

    def shift_split(d):
        edge = position(d) == COUNT[d] - 1
        for order, nu in enumerate(others(d)):
            base = slot(d, nu) * 18
            got = {}
            for part in range(2):
                for i in range(2):
                    for j in range(3):
                        where = order * 12 + (part * 2 + i) * 3 + j
                        local = turn(u[comp(nu, part, i, j)], d, -1)
                        value = jnp.where(edge, unpack(recv1[d], where, d, high=True), local)
                        got[part, i, j] = value
                        shifted[base + part * 9 + i * 3 + j] = value
            for j in range(3):
                p, q = (j + 1) % 3, (j + 2) % 3
                r0p, r0q, r1p, r1q = got[0, 0, p], got[0, 0, q], got[0, 1, p], got[0, 1, q]
                i0p, i0q, i1p, i1q = got[1, 0, p], got[1, 0, q], got[1, 1, p], got[1, 1, q]
                shifted[base + 6 + j] = r0p * r1q - i0p * i1q - r0q * r1p + i0q * i1p
                shifted[base + 15 + j] = r0q * i1p + i0q * r1p - r0p * i1q - i0p * r1q

    seen = set()

    def do_plane(plane, mu, nu):
        fresh_mu, fresh_nu = mu not in seen, nu not in seen
        seen.update((mu, nu))

        def body(v, carry):
            rows = pl.ds(pl.multiple_of(v * 8, 8), 8)

            def get(ref, base, i, j):
                return (ref[base + i * 3 + j, rows, :], ref[base + 9 + i * 3 + j, rows, :])

            cbase = slot(mu, nu) * 18
            dbase = slot(nu, mu) * 18
            t = [[None] * 3 for _ in range(3)]
            for i in range(3):
                ci = [get(shifted, cbase, i, k) for k in range(3)]
                for j in range(3):
                    t[i][j] = dot3([(ci[k], get(shifted, dbase, j, k)) for k in range(3)], conj_b=True)

            x = [[None] * 3 for _ in range(3)]
            for i in range(3):
                ai = [get(u, mu * 18, i, k) for k in range(3)]
                for j in range(3):
                    x[i][j] = dot3([(ai[k], t[k][j]) for k in range(3)])

            def p_entry(i, j, parts):
                return dot3([(x[i][k], get(u, nu * 18, j, k)) for k in range(3)], conj_b=True, parts=parts)

            diag = [p_entry(i, i, "i")[1] for i in range(3)]
            trace = (diag[0] + diag[1] + diag[2]) * (1.0 / 3.0)
            values = leaf(lambda i, j, parts: (None, diag[i]) if i == j else p_entry(i, j, parts), trace)
            for c in range(8):
                at_mu = (mu * 8 + c, rows, slice(None))
                at_nu = (nu * 8 + c, rows, slice(None))
                if fresh_mu:
                    store[at_mu] = values[c]
                else:
                    store[at_mu] = store[at_mu] + values[c]
                if fresh_nu:
                    store[at_nu] = -values[c]
                else:
                    store[at_nu] = store[at_nu] - values[c]

            def w(i, j):
                return get(wmat, plane * 18, i, j)

            values = leaf(lambda i, j, parts: dot3([(w(i, k), t[k][j]) for k in range(3)], parts=parts), trace)
            for c in range(8):
                leaves[slot(nu, mu) * 8 + c, rows, :] = values[c]
            values = leaf(lambda i, j, parts: dot3([(t[i][k], w(k, j)) for k in range(3)], parts=parts), trace)
            for c in range(8):
                leaves[slot(mu, nu) * 8 + c, rows, :] = values[c]
            return carry

        lax.fori_loop(0, 2, body, 0)

    shift_x()
    for plane, (mu, nu) in enumerate(PLANES):
        make_w(plane, mu, nu)
    down[2].wait_recv()
    shift_split(2)
    do_plane(1, 2, 3)
    down[0].wait_recv()
    shift_split(0)
    do_plane(0, 0, 3)
    do_plane(2, 0, 2)
    down[1].wait_recv()
    shift_split(1)
    do_plane(3, 1, 3)
    do_plane(4, 1, 2)
    do_plane(5, 0, 1)

    up = [
        pltpu.make_async_remote_copy(
            src_ref=send2[d], dst_ref=recv2[d], send_sem=s2.at[d], recv_sem=r2.at[d],
            device_id=above[d], device_id_type=MESH,
        )
        for d in range(3)
    ]

    def leaf_at(index):
        return lambda: leaves[index]

    for d in (1, 0, 2):
        pack([leaf_at(slot(d, nu) * 8 + c) for nu in others(d) for c in range(8)], send2[d], d, high=True)
    for d in (1, 0, 2):
        up[d].start()

    def sign(d, nu):
        return -1 if (nu, d) in PLANES else 1

    def add(at, value, positive):
        store[at] = store[at] + value if positive else store[at] - value

    first = position(3) == 0
    for nu in others(3):
        for c in range(8):
            value = leaves[slot(3, nu) * 8 + c]
            value = jnp.where(first, pltpu.roll(value, LANES - NX + 1, axis=1), pltpu.roll(value, 1, axis=1))
            add(nu * 8 + c, value, sign(3, nu) > 0)
    for d in (2, 0, 1):
        up[d].wait_recv()
        first = position(d) == 0
        for order, nu in enumerate(others(d)):
            for c in range(8):
                value = turn(leaves[slot(d, nu) * 8 + c], d, 1)
                value = jnp.where(first, unpack(recv2[d], order * 8 + c, d, high=False), value)
                add(nu * 8 + c, value, sign(d, nu) > 0)

    for mu in range(4):
        for number, (i, j) in enumerate(OFF):
            real = store[mu * 8 + number * 2] * (0.5 * COEFF)
            imag = store[mu * 8 + number * 2 + 1] * (0.5 * COEFF)
            out_ref[comp(mu, 0, i, j)] = real
            out_ref[comp(mu, 0, j, i)] = -real
            out_ref[comp(mu, 1, i, j)] = imag
            out_ref[comp(mu, 1, j, i)] = imag
        diag0 = store[mu * 8 + 6] * COEFF
        diag1 = store[mu * 8 + 7] * COEFF
        for i, value in enumerate((diag0, diag1, -(diag0 + diag1))):
            out_ref[comp(mu, 1, i, i)] = value
            out_ref[comp(mu, 0, i, i)] = jnp.zeros_like(value)

    for d in range(3):
        down[d].wait_send()
        up[d].wait_send()


def per_device(links):
    shape = links.shape
    vmem = pltpu.VMEM
    counts1 = [-(-36 // g) for g in GROUP]
    counts2 = [24 // g for g in GROUP]

    def packed(counts):
        return [vmem((n, ROWS, LANES), jnp.float32) for n in counts]

    out = pl.pallas_call(
        kernel,
        out_shape=jax.ShapeDtypeStruct((72, ROWS, LANES), jnp.float32),
        in_specs=[pl.BlockSpec(memory_space=pl.ANY)],
        out_specs=pl.BlockSpec(memory_space=pltpu.VMEM),
        scratch_shapes=[
            vmem((72, ROWS, LANES), jnp.float32),
            vmem((216, ROWS, LANES), jnp.float32),
            vmem((32, ROWS, LANES), jnp.float32),
            vmem((96, ROWS, LANES), jnp.float32),
            vmem((108, ROWS, LANES), jnp.float32),
            packed(counts1),
            packed(counts1),
            packed(counts2),
            packed(counts2),
            pltpu.SemaphoreType.DMA((4,)),
            pltpu.SemaphoreType.DMA((3,)),
            pltpu.SemaphoreType.DMA((3,)),
            pltpu.SemaphoreType.DMA((3,)),
            pltpu.SemaphoreType.DMA((3,)),
        ],
        compiler_params=pltpu.CompilerParams(collective_id=0, has_side_effects=True),
    )(links.reshape(72, ROWS, LANES))
    return out.reshape(shape)


def solution(mesh):
    return jax.shard_map(
        per_device,
        mesh=mesh,
        in_specs=(P(None, None, None, None, "ta", "gz", "gx"),),
        out_specs=P(None, None, None, None, "ta", "gz", "gx"),
        check_vma=False,
    )
```

time: 70.4 us -> 22.3 us (0.32)
  the two profiles are of different devices: /device:TPU:6 before, /device:TPU:1 now
where the time goes in v1:
time: 22.3 us; the launch traced here: 22.2 us
  Pallas kernels  20.2 us (91%)
  local copies, waits for them, and re-layouts  1.92 us (9%)
    pallas_call x1, Pallas kernels, per_device(): pl.pallas_call(kernel, out_shape=jax.ShapeDtypeStruct((72, ROWS, LANES),...  20.2 us
    unnamed x1, local copies, waits for them, and re-layouts  1.92 us

profile of v1, /device:TPU:1, one launch (start us, length us, event | category | flops | bytes accessed | tf_op | source)
XLA Modules:
  0.0 22.2 jit_solution(9676486429141994957)
XLA Ops:
  0.0 20.2 %shard_map.17 = f32[72,16,128]{2,1,0:T(8,128)} custom-call(f32[72,16,128]{2,1,0:T(8,128)} %bitcast.3), custom_call_target="tpu_custom_call" | custom-call | tf_op jit(solution)/shard_map/pallas_call | solution.py:336
  20.3 1.9 %copy.3 = f32[4,2,3,3,4,4,128]{6,5,4,3,2,1,0:T(4,128)} copy(f32[4,2,3,3,4,4,128]{6,5,4,3,2,1,0:T(4,128)} %bitcast.2) | data formatting | bytes 1179648

commit v2 on v1

--- a/solution.py
+++ b/solution.py
@@ -63,11 +63,37 @@
     return turn(buf[index // width], direction, width - 1 - j if high else -j)
 
 
-def cmul(a, b, conj_a=False, conj_b=False):
-    (ar, ai), (br, bi) = a, b
-    sa = -1 if conj_a else 1
-    sb = -1 if conj_b else 1
-    return ([(1, ar * br), (-sa * sb, ai * bi)], [(sb, ar * bi), (sa, ai * br)])
+def edge_place(d, e, c):
+    return (c // 8, c % 8) if e == 2 else (c % 4, c // 4)
+
+
+def pack_edge(loads, buf, d, e):
+    packed = None
+    for c, load in enumerate(loads):
+        at_d, at_e = edge_place(d, e, c)
+        moved = turn(turn(load(), d, at_d - (COUNT[d] - 1)), e, at_e)
+        here = (position(d) == at_d) & (position(e) == at_e)
+        packed = moved if packed is None else jnp.where(here, moved, packed)
+    buf[...] = packed
+
+
+def unpack_edge(buf, d, e, c, to_d):
+    at_d, at_e = edge_place(d, e, c)
+    return turn(turn(buf[...], d, to_d - at_d), e, COUNT[e] - 1 - at_e)
+
+
+def shift_within_x(value):
+    edge = position(3) == NX - 1
+    return jnp.where(edge, pltpu.roll(value, NX - 1, axis=1), pltpu.roll(value, LANES - 1, axis=1))
+
+
+def third_row(get, put):
+    for j in range(3):
+        p, q = (j + 1) % 3, (j + 2) % 3
+        r0p, r0q, r1p, r1q = get(0, 0, p), get(0, 0, q), get(0, 1, p), get(0, 1, q)
+        i0p, i0q, i1p, i1q = get(1, 0, p), get(1, 0, q), get(1, 1, p), get(1, 1, q)
+        put(0, j, r0p * r1q - i0p * i1q - r0q * r1p + i0q * i1p)
+        put(1, j, r0q * i1p + i0q * r1p - r0p * i1q - i0p * r1q)
 
 
 def total(terms):
@@ -109,8 +135,35 @@
     return values
 
 
-def kernel(links_ref, out_ref, u, shifted, store, leaves, wmat, send1, recv1, send2, recv2,
-           in_sem, s1, r1, s2, r2):
+FACES = (0, 1)
+EDGES = ((0, 1), (0, 2), (1, 0), (1, 2))
+OUTGOING = (
+    [tuple(-1 if k == d else 0 for k in range(3)) for d in range(3)]
+    + [tuple(1 if k == d else 0 for k in range(3)) for d in range(3)]
+    + [tuple(1 if k == d else -1 if k == e else 0 for k in range(3)) for d, e in EDGES]
+)
+TWO_ROWS = [(part, i, j) for part in range(2) for i in range(2) for j in range(3)]
+
+
+def kernel(links_ref, out_ref, u, shifted, store, leaves, wmat, send1, recv1, send2, recv2, sende, recve,
+           near, far, base, moved, faceleaf, in_sem, s1, r1, s2, r2, se, re):
+    index = [lax.axis_index(name) for name in RING]
+    size = [lax.axis_size(name) for name in RING]
+    first_time = index[0] == 0
+    last_time = index[0] == size[0] - 1
+
+    def device(offset, back=False):
+        return {
+            RING[k]: lax.rem(index[k] + size[k] + (-step if back else step), size[k])
+            for k, step in enumerate(offset)
+            if step
+        }
+
+    barrier = pltpu.get_barrier_semaphore()
+
+    def greet(offset):
+        pl.semaphore_signal(barrier, inc=1, device_id=device(offset, back=True), device_id_type=MESH)
+
     fetch = [
         pltpu.make_async_copy(links_ref.at[pl.ds(mu * 18, 18)], u.at[pl.ds(mu * 18, 18)], in_sem.at[mu])
         for mu in range(4)
@@ -118,33 +171,73 @@
     for copy in fetch:
         copy.start()
 
-    index = [lax.axis_index(name) for name in RING]
-    size = [lax.axis_size(name) for name in RING]
-    below = [{RING[d]: lax.rem(index[d] + size[d] - 1, size[d])} for d in range(3)]
-    above = [{RING[d]: lax.rem(index[d] + 1, size[d])} for d in range(3)]
-    barrier = pltpu.get_barrier_semaphore()
-    for d in (1, 0, 2):
-        pl.semaphore_signal(barrier, inc=1, device_id=below[d], device_id_type=MESH)
-        pl.semaphore_signal(barrier, inc=1, device_id=above[d], device_id_type=MESH)
+    for offset in OUTGOING:
+        if offset[0] == 0:
+            greet(offset)
+
+    @pl.when(jnp.logical_not(first_time))
+    def _():
+        for offset in OUTGOING:
+            if offset[0] == 1:
+                greet(offset)
+
+    @pl.when(jnp.logical_not(last_time))
+    def _():
+        for offset in OUTGOING:
+            if offset[0] == -1:
+                greet(offset)
+
     for copy in fetch:
         copy.wait()
 
     def link(mu, part, i, j):
         return lambda: u[comp(mu, part, i, j)]
 
+    for d in FACES:
+        pack([link(nu, *c) for c in TWO_ROWS for nu in others(d) + [d]], send2[d], d, high=True)
+    for number, (d, e) in enumerate(EDGES):
+        pack_edge([link(d, *c) for c in TWO_ROWS], sende[number], d, e)
     for d in (1, 0, 2):
-        loads = [link(nu, part, i, j) for nu in others(d) for part in range(2) for i in range(2) for j in range(3)]
-        pack(loads, send1[d], d, high=False)
-    pl.semaphore_wait(barrier, 6)
-    down = [
-        pltpu.make_async_remote_copy(
-            src_ref=send1[d], dst_ref=recv1[d], send_sem=s1.at[d], recv_sem=r1.at[d],
-            device_id=below[d], device_id_type=MESH,
+        pack([link(nu, *c) for nu in others(d) for c in TWO_ROWS], send1[d], d, high=False)
+
+    down_time = [offset for offset in OUTGOING if offset[0] == -1]
+
+    @pl.when(first_time)
+    def _():
+        pl.semaphore_wait(barrier, len(OUTGOING) - len(down_time))
+        for offset in OUTGOING:
+            if offset[0] == 1:
+                greet(offset)
+
+    @pl.when(jnp.logical_not(first_time))
+    def _():
+        pl.semaphore_wait(barrier, len(OUTGOING))
+
+    @pl.when(last_time)
+    def _():
+        for offset in down_time:
+            greet(offset)
+
+    def remote(src, dst, send, recv, offset):
+        return pltpu.make_async_remote_copy(
+            src_ref=src, dst_ref=dst, send_sem=send, recv_sem=recv,
+            device_id=device(offset), device_id_type=MESH,
         )
-        for d in range(3)
-    ]
-    for d in (1, 0, 2):
-        down[d].start()
+
+    down = [remote(send1[d], recv1[d], s1.at[d], r1.at[d], OUTGOING[d]) for d in range(3)]
+    up = [remote(send2[d], recv2[d], s2.at[d], r2.at[d], OUTGOING[3 + d]) for d in range(3)]
+    corner = [remote(sende[n], recve[n], se.at[n], re.at[n], OUTGOING[6 + n]) for n in range(4)]
+    up[0].start()
+    up[1].start()
+    down[1].start()
+    down[2].start()
+    for n in (0, 1, 3):
+        corner[n].start()
+
+    @pl.when(jnp.logical_not(first_time))
+    def _():
+        down[0].start()
+        corner[2].start()
 
     def make_w(plane, mu, nu):
         def body(v, carry):
@@ -166,34 +259,95 @@
         lax.fori_loop(0, 2, body, 0)
 
     def shift_x():
-        edge = position(3) == NX - 1
         for nu in others(3):
-            base = slot(3, nu) * 18
+            at = slot(3, nu) * 18
             for c in range(18):
-                value = u[nu * 18 + c]
-                shifted[base + c] = jnp.where(
-                    edge, pltpu.roll(value, NX - 1, axis=1), pltpu.roll(value, LANES - 1, axis=1)
-                )
+                shifted[at + c] = shift_within_x(u[nu * 18 + c])
 
     def shift_split(d):
         edge = position(d) == COUNT[d] - 1
         for order, nu in enumerate(others(d)):
-            base = slot(d, nu) * 18
+            at = slot(d, nu) * 18
             got = {}
-            for part in range(2):
-                for i in range(2):
-                    for j in range(3):
-                        where = order * 12 + (part * 2 + i) * 3 + j
-                        local = turn(u[comp(nu, part, i, j)], d, -1)
-                        value = jnp.where(edge, unpack(recv1[d], where, d, high=True), local)
-                        got[part, i, j] = value
-                        shifted[base + part * 9 + i * 3 + j] = value
+            for number, (part, i, j) in enumerate(TWO_ROWS):
+                local = turn(u[comp(nu, part, i, j)], d, -1)
+                value = jnp.where(edge, unpack(recv1[d], order * 12 + number, d, high=True), local)
+                got[part, i, j] = value
+                shifted[at + part * 9 + i * 3 + j] = value
+
+            def put(part, j, value, at=at):
+                shifted[at + part * 9 + 6 + j] = value
+
+            third_row(lambda *c: got[c], put)
+
+    def face_near(d):
+        where = position(d)
+        for c in range(18):
+            value = None
+            for j, nu in enumerate(others(d)):
+                part = turn(u[nu * 18 + c], d, j)
+                value = part if value is None else jnp.where(where == j, part, value)
+            near[d * 18 + c] = value
+
+    def face_leaf(d):
+        where = position(d)
+        got_far, got_base, got_moved = {}, {}, {}
+        for number, c in enumerate(TWO_ROWS):
+            value = recv2[d][number]
+            got_far[c] = value
+            spread = value
             for j in range(3):
-                p, q = (j + 1) % 3, (j + 2) % 3
-                r0p, r0q, r1p, r1q = got[0, 0, p], got[0, 0, q], got[0, 1, p], got[0, 1, q]
-                i0p, i0q, i1p, i1q = got[1, 0, p], got[1, 0, q], got[1, 1, p], got[1, 1, q]
-                shifted[base + 6 + j] = r0p * r1q - i0p * i1q - r0q * r1p + i0q * i1p
-                shifted[base + 15 + j] = r0q * i1p + i0q * r1p - r0p * i1q - i0p * r1q
+                spread = jnp.where(where == j, turn(value, d, j - 3), spread)
+            got_base[c] = spread
+            shift = shift_within_x(spread)
+            for j, mu in enumerate(others(d)):
+                if mu == 3:
+                    continue
+                edge = EDGES.index((d, mu))
+                step = jnp.where(
+                    position(mu) == COUNT[mu] - 1,
+                    unpack_edge(recve[edge], d, mu, number, j),
+                    turn(spread, mu, -1),
+                )
+                shift = jnp.where(where == j, step, shift)
+            got_moved[c] = shift
+        for ref, got in ((far, got_far), (base, got_base), (moved, got_moved)):
+            for (part, i, j), value in got.items():
+                ref[part * 9 + i * 3 + j] = value
+
+            def put(part, j, value, ref=ref):
+                ref[part * 9 + 6 + j] = value
+
+            third_row(lambda *c: got[c], put)
+
+        def body(v, carry):
+            rows = pl.ds(pl.multiple_of(v * 8, 8), 8)
+
+            def get(ref, at, i, j):
+                return (ref[at + i * 3 + j, rows, :], ref[at + 9 + i * 3 + j, rows, :])
+
+            g = [[None] * 3 for _ in range(3)]
+            for i in range(3):
+                hi = [get(far, 0, i, k) for k in range(3)]
+                for j in range(3):
+                    g[i][j] = dot3([(hi[k], get(moved, 0, k, j)) for k in range(3)])
+            x = [[None] * 3 for _ in range(3)]
+            for i in range(3):
+                ai = [get(near, d * 18, i, k) for k in range(3)]
+                for j in range(3):
+                    x[i][j] = dot3([(ai[k], g[j][k]) for k in range(3)], conj_b=True)
+
+            def entry(i, j, parts):
+                return dot3([(x[i][k], get(base, 0, k, j)) for k in range(3)], parts=parts)
+
+            diag = [entry(i, i, "i")[1] for i in range(3)]
+            trace = (diag[0] + diag[1] + diag[2]) * (1.0 / 3.0)
+            values = leaf(lambda i, j, parts: (None, diag[i]) if i == j else entry(i, j, parts), trace)
+            for c in range(8):
+                faceleaf[c, rows, :] = values[c]
+            return carry
+
+        lax.fori_loop(0, 2, body, 0)
 
     seen = set()
 
@@ -255,34 +409,32 @@
     shift_x()
     for plane, (mu, nu) in enumerate(PLANES):
         make_w(plane, mu, nu)
+    for d in FACES:
+        face_near(d)
     down[2].wait_recv()
     shift_split(2)
     do_plane(1, 2, 3)
+    down[1].wait_recv()
+    shift_split(1)
+    do_plane(4, 1, 2)
+    do_plane(3, 1, 3)
     down[0].wait_recv()
     shift_split(0)
-    do_plane(0, 0, 3)
     do_plane(2, 0, 2)
-    down[1].wait_recv()
-    shift_split(1)
-    do_plane(3, 1, 3)
-    do_plane(4, 1, 2)
-    do_plane(5, 0, 1)
-
-    up = [
-        pltpu.make_async_remote_copy(
-            src_ref=send2[d], dst_ref=recv2[d], send_sem=s2.at[d], recv_sem=r2.at[d],
-            device_id=above[d], device_id_type=MESH,
-        )
-        for d in range(3)
-    ]
 
     def leaf_at(index):
         return lambda: leaves[index]
 
-    for d in (1, 0, 2):
-        pack([leaf_at(slot(d, nu) * 8 + c) for nu in others(d) for c in range(8)], send2[d], d, high=True)
-    for d in (1, 0, 2):
-        up[d].start()
+    pack([leaf_at(slot(2, nu) * 8 + c) for nu in others(2) for c in range(8)], send2[2], 2, high=True)
+    do_plane(0, 0, 3)
+    up[2].start()
+    do_plane(5, 0, 1)
+
+    @pl.when(first_time)
+    def _():
+        pl.semaphore_wait(barrier, len(down_time))
+        down[0].start()
+        corner[2].start()
 
     def sign(d, nu):
         return -1 if (nu, d) in PLANES else 1
@@ -296,14 +448,25 @@
             value = leaves[slot(3, nu) * 8 + c]
             value = jnp.where(first, pltpu.roll(value, LANES - NX + 1, axis=1), pltpu.roll(value, 1, axis=1))
             add(nu * 8 + c, value, sign(3, nu) > 0)
-    for d in (2, 0, 1):
+    up[2].wait_recv()
+    first = position(2) == 0
+    for order, nu in enumerate(others(2)):
+        for c in range(8):
+            value = turn(leaves[slot(2, nu) * 8 + c], 2, 1)
+            value = jnp.where(first, unpack(recv2[2], order * 8 + c, 2, high=False), value)
+            add(nu * 8 + c, value, sign(2, nu) > 0)
+    for d in (1, 0):
         up[d].wait_recv()
+        for n, (first, _) in enumerate(EDGES):
+            if first == d:
+                corner[n].wait_recv()
+        face_leaf(d)
         first = position(d) == 0
         for order, nu in enumerate(others(d)):
             for c in range(8):
                 value = turn(leaves[slot(d, nu) * 8 + c], d, 1)
-                value = jnp.where(first, unpack(recv2[d], order * 8 + c, d, high=False), value)
-                add(nu * 8 + c, value, sign(d, nu) > 0)
+                edge = turn(faceleaf[c], d, -order)
+                add(nu * 8 + c, jnp.where(first, edge if sign(d, nu) > 0 else -edge, value), sign(d, nu) > 0)
 
     for mu in range(4):
         for number, (i, j) in enumerate(OFF):
@@ -319,43 +482,35 @@
             out_ref[comp(mu, 1, i, i)] = value
             out_ref[comp(mu, 0, i, i)] = jnp.zeros_like(value)
 
-    for d in range(3):
-        down[d].wait_send()
-        up[d].wait_send()
+    for copy in down + up + corner:
+        copy.wait_send()
 
 
 def per_device(links):
     shape = links.shape
     vmem = pltpu.VMEM
-    counts1 = [-(-36 // g) for g in GROUP]
-    counts2 = [24 // g for g in GROUP]
 
     def packed(counts):
         return [vmem((n, ROWS, LANES), jnp.float32) for n in counts]
 
+    counts1 = [-(-36 // g) for g in GROUP]
+    counts2 = (12, 12, 3)
+    edges = [vmem((ROWS, LANES), jnp.float32) for _ in EDGES]
+    arrays = (72, 216, 32, 96, 108)
+    dma = pltpu.SemaphoreType.DMA
     out = pl.pallas_call(
         kernel,
         out_shape=jax.ShapeDtypeStruct((72, ROWS, LANES), jnp.float32),
-        in_specs=[pl.BlockSpec(memory_space=pl.ANY)],
+        in_specs=[pl.BlockSpec(memory_space=pltpu.HBM)],
         out_specs=pl.BlockSpec(memory_space=pltpu.VMEM),
-        scratch_shapes=[
-            vmem((72, ROWS, LANES), jnp.float32),
-            vmem((216, ROWS, LANES), jnp.float32),
-            vmem((32, ROWS, LANES), jnp.float32),
-            vmem((96, ROWS, LANES), jnp.float32),
-            vmem((108, ROWS, LANES), jnp.float32),
-            packed(counts1),
-            packed(counts1),
-            packed(counts2),
-            packed(counts2),
-            pltpu.SemaphoreType.DMA((4,)),
-            pltpu.SemaphoreType.DMA((3,)),
-            pltpu.SemaphoreType.DMA((3,)),
-            pltpu.SemaphoreType.DMA((3,)),
-            pltpu.SemaphoreType.DMA((3,)),
-        ],
-        compiler_params=pltpu.CompilerParams(collective_id=0, has_side_effects=True),
-    )(links.reshape(72, ROWS, LANES))
+        scratch_shapes=packed(arrays)
+        + [packed(counts1), packed(counts1), packed(counts2), packed(counts2), edges, edges]
+        + packed((36, 18, 18, 18, 8))
+        + [dma((n,)) for n in (4, 3, 3, 3, 3, 4, 4)],
+        compiler_params=pltpu.CompilerParams(
+            collective_id=0, has_side_effects=True, vmem_limit_bytes=16 * 1024 * 1024
+        ),
+    )(pltpu.with_memory_space_constraint(links.reshape(72, ROWS, LANES), pltpu.HBM))
     return out.reshape(shape)
 
 

time: 22.3 us -> 17.5 us (0.78)
  the two profiles are of different devices: /device:TPU:1 before, /device:TPU:224 now
where the time goes in v2:
time: 17.5 us; the launch traced here: 17.4 us
  Pallas kernels  16.6 us (95%)
  local copies, waits for them, and re-layouts  0.82 us (5%)
    pallas_call x1, Pallas kernels, per_device(): pl.pallas_call(kernel, out_shape=jax.ShapeDtypeStruct((72, ROWS, LANES),...  16.6 us
    unnamed x1, local copies, waits for them, and re-layouts  0.82 us

profile of v2, /device:TPU:224, one launch (start us, length us, event | category | flops | bytes accessed | tf_op | source)
XLA Modules:
  0.0 17.4 jit_solution(12653207893110171282)
XLA Ops:
  0.0 16.6 %shard_map.17 = f32[72,16,128]{2,1,0:T(8,128)S(1)} custom-call(f32[72,16,128]{2,1,0:T(8,128)} %bitcast.3), custom_call_target="tpu_custom_call" | custom-call | tf_op jit(solution)/shard_map/pallas_call | solution.py:501
  16.6 0.8 %copy.3 = f32[4,2,3,3,4,4,128]{6,5,4,3,2,1,0:T(4,128)} copy(f32[4,2,3,3,4,4,128]{6,5,4,3,2,1,0:T(4,128)S(1)} %bitcast.2) | data formatting | bytes 1179648

commit v3 on v2

--- a/solution.py
+++ b/solution.py
@@ -135,13 +135,21 @@
     return values
 
 
-FACES = (0, 1)
-EDGES = ((0, 1), (0, 2), (1, 0), (1, 2))
-OUTGOING = (
-    [tuple(-1 if k == d else 0 for k in range(3)) for d in range(3)]
-    + [tuple(1 if k == d else 0 for k in range(3)) for d in range(3)]
-    + [tuple(1 if k == d else -1 if k == e else 0 for k in range(3)) for d, e in EDGES]
-)
+FACES = (0, 1, 2)
+EDGES = ((0, 1), (0, 2), (1, 0), (1, 2), (2, 0), (2, 1))
+
+
+def offset_of(plus=None, minus=None):
+    return tuple(1 if k == plus else -1 if k == minus else 0 for k in range(3))
+
+
+DOWN = [offset_of(minus=d) for d in range(3)]
+UP = [offset_of(plus=d) for d in range(3)]
+CORNER = [offset_of(d, e) for d, e in EDGES]
+DIRECT = [EDGES.index(pair) for pair in ((1, 0), (1, 2), (2, 0))]
+OUTGOING = DOWN + UP + [CORNER[n] for n in DIRECT]
+WRAP_LATER = [CORNER[EDGES.index(pair)] for pair in ((1, 0), (2, 0))]
+WRAP_SOONER = [CORNER[EDGES.index(pair)] for pair in ((0, 1), (0, 2))]
 TWO_ROWS = [(part, i, j) for part in range(2) for i in range(2) for j in range(3)]
 
 
@@ -172,20 +180,18 @@
         copy.start()
 
     for offset in OUTGOING:
-        if offset[0] == 0:
+        if offset not in WRAP_LATER:
             greet(offset)
-
-    @pl.when(jnp.logical_not(first_time))
-    def _():
-        for offset in OUTGOING:
-            if offset[0] == 1:
-                greet(offset)
 
     @pl.when(jnp.logical_not(last_time))
     def _():
-        for offset in OUTGOING:
-            if offset[0] == -1:
-                greet(offset)
+        for offset in WRAP_LATER:
+            greet(offset)
+
+    @pl.when(first_time)
+    def _():
+        for offset in WRAP_SOONER:
+            greet(offset)
 
     for copy in fetch:
         copy.wait()
@@ -200,23 +206,17 @@
     for d in (1, 0, 2):
         pack([link(nu, *c) for nu in others(d) for c in TWO_ROWS], send1[d], d, high=False)
 
-    down_time = [offset for offset in OUTGOING if offset[0] == -1]
-
     @pl.when(first_time)
     def _():
-        pl.semaphore_wait(barrier, len(OUTGOING) - len(down_time))
-        for offset in OUTGOING:
-            if offset[0] == 1:
-                greet(offset)
-
-    @pl.when(jnp.logical_not(first_time))
+        pl.semaphore_wait(barrier, len(OUTGOING) - len(WRAP_LATER))
+
+    @pl.when(last_time)
+    def _():
+        pl.semaphore_wait(barrier, len(OUTGOING) + len(WRAP_SOONER))
+
+    @pl.when(jnp.logical_not(first_time | last_time))
     def _():
         pl.semaphore_wait(barrier, len(OUTGOING))
-
-    @pl.when(last_time)
-    def _():
-        for offset in down_time:
-            greet(offset)
 
     def remote(src, dst, send, recv, offset):
         return pltpu.make_async_remote_copy(
@@ -224,20 +224,29 @@
             device_id=device(offset), device_id_type=MESH,
         )
 
-    down = [remote(send1[d], recv1[d], s1.at[d], r1.at[d], OUTGOING[d]) for d in range(3)]
-    up = [remote(send2[d], recv2[d], s2.at[d], r2.at[d], OUTGOING[3 + d]) for d in range(3)]
-    corner = [remote(sende[n], recve[n], se.at[n], re.at[n], OUTGOING[6 + n]) for n in range(4)]
+    down = [remote(send1[d], recv1[d], s1.at[d], r1.at[d], DOWN[d]) for d in range(3)]
+    up = [remote(send2[d], recv2[d], s2.at[d], r2.at[d], UP[d]) for d in range(3)]
+    corner = {
+        pair: remote(sende[n], recve[n], se.at[n], re.at[n], CORNER[n]) for n, pair in enumerate(EDGES)
+    }
+    down[2].start()
     up[0].start()
+    down[0].start()
     up[1].start()
     down[1].start()
-    down[2].start()
-    for n in (0, 1, 3):
-        corner[n].start()
+    up[2].start()
+    corner[1, 2].start()
+
+    def start_up_time():
+        corner[0, 1].start()
+        corner[0, 2].start()
+
+    pl.when(last_time)(start_up_time)
 
     @pl.when(jnp.logical_not(first_time))
     def _():
-        down[0].start()
-        corner[2].start()
+        corner[1, 0].start()
+        corner[2, 0].start()
 
     def make_w(plane, mu, nu):
         def body(v, carry):
@@ -292,8 +301,9 @@
     def face_leaf(d):
         where = position(d)
         got_far, got_base, got_moved = {}, {}, {}
+        per_tile = GROUP[d] // 4
         for number, c in enumerate(TWO_ROWS):
-            value = recv2[d][number]
+            value = turn(recv2[d][number // per_tile], d, -4 * (number % per_tile))
             got_far[c] = value
             spread = value
             for j in range(3):
@@ -412,61 +422,49 @@
     for d in FACES:
         face_near(d)
     down[2].wait_recv()
+    corner[2, 1].start()
+    pl.when(first_time)(corner[2, 0].start)
     shift_split(2)
     do_plane(1, 2, 3)
+    down[0].wait_recv()
+    pl.when(jnp.logical_not(last_time))(start_up_time)
+    shift_split(0)
+    do_plane(0, 0, 3)
+    do_plane(2, 0, 2)
     down[1].wait_recv()
+    pl.when(first_time)(corner[1, 0].start)
     shift_split(1)
+    do_plane(3, 1, 3)
     do_plane(4, 1, 2)
-    do_plane(3, 1, 3)
-    down[0].wait_recv()
-    shift_split(0)
-    do_plane(2, 0, 2)
-
-    def leaf_at(index):
-        return lambda: leaves[index]
-
-    pack([leaf_at(slot(2, nu) * 8 + c) for nu in others(2) for c in range(8)], send2[2], 2, high=True)
-    do_plane(0, 0, 3)
-    up[2].start()
     do_plane(5, 0, 1)
-
-    @pl.when(first_time)
-    def _():
-        pl.semaphore_wait(barrier, len(down_time))
-        down[0].start()
-        corner[2].start()
 
     def sign(d, nu):
         return -1 if (nu, d) in PLANES else 1
 
-    def add(at, value, positive):
-        store[at] = store[at] + value if positive else store[at] - value
-
-    first = position(3) == 0
-    for nu in others(3):
+    for nu in range(4):
         for c in range(8):
-            value = leaves[slot(3, nu) * 8 + c]
-            value = jnp.where(first, pltpu.roll(value, LANES - NX + 1, axis=1), pltpu.roll(value, 1, axis=1))
-            add(nu * 8 + c, value, sign(3, nu) > 0)
-    up[2].wait_recv()
-    first = position(2) == 0
-    for order, nu in enumerate(others(2)):
-        for c in range(8):
-            value = turn(leaves[slot(2, nu) * 8 + c], 2, 1)
-            value = jnp.where(first, unpack(recv2[2], order * 8 + c, 2, high=False), value)
-            add(nu * 8 + c, value, sign(2, nu) > 0)
-    for d in (1, 0):
+            value = store[nu * 8 + c]
+            for d in others(nu):
+                moved_leaf = leaves[slot(d, nu) * 8 + c]
+                first = position(d) == 0
+                if d == 3:
+                    around = pltpu.roll(moved_leaf, LANES - NX + 1, axis=1)
+                    moved_leaf = jnp.where(first, around, pltpu.roll(moved_leaf, 1, axis=1))
+                else:
+                    moved_leaf = jnp.where(first, 0.0, turn(moved_leaf, d, 1))
+                value = value + moved_leaf if sign(d, nu) > 0 else value - moved_leaf
+            store[nu * 8 + c] = value
+
+    for d in (2, 1, 0):
         up[d].wait_recv()
-        for n, (first, _) in enumerate(EDGES):
-            if first == d:
-                corner[n].wait_recv()
+        for pair in EDGES:
+            if pair[0] == d:
+                corner[pair].wait_recv()
         face_leaf(d)
         first = position(d) == 0
         for order, nu in enumerate(others(d)):
             for c in range(8):
-                value = turn(leaves[slot(d, nu) * 8 + c], d, 1)
-                edge = turn(faceleaf[c], d, -order)
-                add(nu * 8 + c, jnp.where(first, edge if sign(d, nu) > 0 else -edge, value), sign(d, nu) > 0)
+                store[nu * 8 + c] += jnp.where(first, turn(faceleaf[c], d, -order), 0.0)
 
     for mu in range(4):
         for number, (i, j) in enumerate(OFF):
@@ -482,7 +480,7 @@
             out_ref[comp(mu, 1, i, i)] = value
             out_ref[comp(mu, 0, i, i)] = jnp.zeros_like(value)
 
-    for copy in down + up + corner:
+    for copy in down + up + list(corner.values()):
         copy.wait_send()
 
 
@@ -494,7 +492,7 @@
         return [vmem((n, ROWS, LANES), jnp.float32) for n in counts]
 
     counts1 = [-(-36 // g) for g in GROUP]
-    counts2 = (12, 12, 3)
+    counts2 = (12, 12, 6)
     edges = [vmem((ROWS, LANES), jnp.float32) for _ in EDGES]
     arrays = (72, 216, 32, 96, 108)
     dma = pltpu.SemaphoreType.DMA
@@ -505,8 +503,8 @@
         out_specs=pl.BlockSpec(memory_space=pltpu.VMEM),
         scratch_shapes=packed(arrays)
         + [packed(counts1), packed(counts1), packed(counts2), packed(counts2), edges, edges]
-        + packed((36, 18, 18, 18, 8))
-        + [dma((n,)) for n in (4, 3, 3, 3, 3, 4, 4)],
+        + packed((54, 18, 18, 18, 8))
+        + [dma((n,)) for n in (4, 3, 3, 3, 3, 6, 6)],
         compiler_params=pltpu.CompilerParams(
             collective_id=0, has_side_effects=True, vmem_limit_bytes=16 * 1024 * 1024
         ),

time: 17.5 us -> 16.8 us (0.960)
  the two profiles are of different devices: /device:TPU:224 before, /device:TPU:1 now
where the time goes in v3:
time: 16.8 us; the launch traced here: 16.7 us
  Pallas kernels  15.9 us (95%)
  local copies, waits for them, and re-layouts  0.82 us (5%)
    pallas_call x1, Pallas kernels, per_device(): pl.pallas_call(kernel, out_shape=jax.ShapeDtypeStruct((72, ROWS, LANES),...  15.9 us
    unnamed x1, local copies, waits for them, and re-layouts  0.82 us

profile of v3, /device:TPU:1, one launch (start us, length us, event | category | flops | bytes accessed | tf_op | source)
XLA Modules:
  0.0 16.7 jit_solution(16858927905441084152)
XLA Ops:
  0.0 15.9 %shard_map.17 = f32[72,16,128]{2,1,0:T(8,128)S(1)} custom-call(f32[72,16,128]{2,1,0:T(8,128)} %bitcast.3), custom_call_target="tpu_custom_call" | custom-call | tf_op jit(solution)/shard_map/pallas_call | solution.py:499
  15.9 0.8 %copy.3 = f32[4,2,3,3,4,4,128]{6,5,4,3,2,1,0:T(4,128)} copy(f32[4,2,3,3,4,4,128]{6,5,4,3,2,1,0:T(4,128)S(1)} %bitcast.2) | data formatting | bytes 1179648

commit v4 on v3

--- a/solution.py
+++ b/solution.py
@@ -146,10 +146,7 @@
 DOWN = [offset_of(minus=d) for d in range(3)]
 UP = [offset_of(plus=d) for d in range(3)]
 CORNER = [offset_of(d, e) for d, e in EDGES]
-DIRECT = [EDGES.index(pair) for pair in ((1, 0), (1, 2), (2, 0))]
-OUTGOING = DOWN + UP + [CORNER[n] for n in DIRECT]
-WRAP_LATER = [CORNER[EDGES.index(pair)] for pair in ((1, 0), (2, 0))]
-WRAP_SOONER = [CORNER[EDGES.index(pair)] for pair in ((0, 1), (0, 2))]
+CORNER_AT = dict(zip(EDGES, CORNER))
 TWO_ROWS = [(part, i, j) for part in range(2) for i in range(2) for j in range(3)]
 
 
@@ -159,6 +156,11 @@
     size = [lax.axis_size(name) for name in RING]
     first_time = index[0] == 0
     last_time = index[0] == size[0] - 1
+    first_z = index[1] == 0
+    last_z = index[1] == size[1] - 1
+
+    def no(condition):
+        return jnp.logical_not(condition)
 
     def device(offset, back=False):
         return {
@@ -179,18 +181,20 @@
     for copy in fetch:
         copy.start()
 
-    for offset in OUTGOING:
-        if offset not in WRAP_LATER:
-            greet(offset)
-
-    @pl.when(jnp.logical_not(last_time))
+    for offset in (DOWN[2], UP[2], CORNER_AT[1, 2]):
+        greet(offset)
+    pl.when(no(first_time))(lambda: greet(UP[0]))
+    pl.when(no(first_z))(lambda: greet(UP[1]))
+    pl.when(no(last_z))(lambda: greet(DOWN[1]))
+
+    @pl.when(no(last_time))
     def _():
-        for offset in WRAP_LATER:
+        for offset in (DOWN[0], CORNER_AT[1, 0], CORNER_AT[2, 0]):
             greet(offset)
 
     @pl.when(first_time)
     def _():
-        for offset in WRAP_SOONER:
+        for offset in (CORNER_AT[0, 1], CORNER_AT[0, 2]):
             greet(offset)
 
     for copy in fetch:
@@ -206,17 +210,14 @@
     for d in (1, 0, 2):
         pack([link(nu, *c) for nu in others(d) for c in TWO_ROWS], send1[d], d, high=False)
 
-    @pl.when(first_time)
-    def _():
-        pl.semaphore_wait(barrier, len(OUTGOING) - len(WRAP_LATER))
-
-    @pl.when(last_time)
-    def _():
-        pl.semaphore_wait(barrier, len(OUTGOING) + len(WRAP_SOONER))
-
-    @pl.when(jnp.logical_not(first_time | last_time))
-    def _():
-        pl.semaphore_wait(barrier, len(OUTGOING))
+    middle = no(first_time | last_time)
+    for here, count in ((first_time, 6), (middle, 9), (last_time, 11)):
+        pl.when(here & first_z)(functools.partial(pl.semaphore_wait, barrier, count - 1))
+        pl.when(here & no(first_z))(functools.partial(pl.semaphore_wait, barrier, count))
+    pl.when(first_time)(lambda: greet(UP[0]))
+    pl.when(first_z)(lambda: greet(UP[1]))
+    pl.when(last_time)(lambda: greet(DOWN[0]))
+    pl.when(last_z)(lambda: greet(DOWN[1]))
 
     def remote(src, dst, send, recv, offset):
         return pltpu.make_async_remote_copy(
@@ -229,24 +230,31 @@
     corner = {
         pair: remote(sende[n], recve[n], se.at[n], re.at[n], CORNER[n]) for n, pair in enumerate(EDGES)
     }
+    def start(*copies):
+        def body():
+            for copy in copies:
+                copy.start()
+
+        return body
+
+    corner[1, 2].start()
+    pl.when(last_time)(start(corner[0, 1], corner[0, 2]))
+    pl.when(no(first_time))(start(corner[1, 0], corner[2, 0]))
     down[2].start()
     up[0].start()
-    down[0].start()
+    pl.when(no(first_time))(down[0].start)
     up[1].start()
-    down[1].start()
+    pl.when(no(first_z))(down[1].start)
     up[2].start()
-    corner[1, 2].start()
-
-    def start_up_time():
-        corner[0, 1].start()
-        corner[0, 2].start()
-
-    pl.when(last_time)(start_up_time)
-
-    @pl.when(jnp.logical_not(first_time))
-    def _():
-        corner[1, 0].start()
-        corner[2, 0].start()
+
+    def second_stage():
+        pl.when(first_time & first_z)(lambda: pl.semaphore_wait(barrier, 2))
+        pl.when(first_time & no(first_z))(lambda: pl.semaphore_wait(barrier, 1))
+        pl.when(no(first_time) & first_z)(lambda: pl.semaphore_wait(barrier, 1))
+        pl.when(first_z)(corner[2, 1].start)
+        pl.when(first_z & no(last_time))(corner[0, 1].start)
+        pl.when(first_z)(down[1].start)
+        pl.when(first_time)(start(corner[1, 0], corner[2, 0], down[0]))
 
     def make_w(plane, mu, nu):
         def body(v, carry):
@@ -359,12 +367,7 @@
 
         lax.fori_loop(0, 2, body, 0)
 
-    seen = set()
-
     def do_plane(plane, mu, nu):
-        fresh_mu, fresh_nu = mu not in seen, nu not in seen
-        seen.update((mu, nu))
-
         def body(v, carry):
             rows = pl.ds(pl.multiple_of(v * 8, 8), 8)
 
@@ -394,14 +397,8 @@
             for c in range(8):
                 at_mu = (mu * 8 + c, rows, slice(None))
                 at_nu = (nu * 8 + c, rows, slice(None))
-                if fresh_mu:
-                    store[at_mu] = values[c]
-                else:
-                    store[at_mu] = store[at_mu] + values[c]
-                if fresh_nu:
-                    store[at_nu] = -values[c]
-                else:
-                    store[at_nu] = store[at_nu] - values[c]
+                store[at_mu] = store[at_mu] + values[c]
+                store[at_nu] = store[at_nu] - values[c]
 
             def w(i, j):
                 return get(wmat, plane * 18, i, j)
@@ -416,46 +413,31 @@
 
         lax.fori_loop(0, 2, body, 0)
 
+    store[...] = jnp.zeros_like(store)
     shift_x()
     for plane, (mu, nu) in enumerate(PLANES):
         make_w(plane, mu, nu)
     for d in FACES:
         face_near(d)
     down[2].wait_recv()
-    corner[2, 1].start()
-    pl.when(first_time)(corner[2, 0].start)
+    pl.when(no(first_z))(corner[2, 1].start)
     shift_split(2)
     do_plane(1, 2, 3)
     down[0].wait_recv()
-    pl.when(jnp.logical_not(last_time))(start_up_time)
+    pl.when(no(last_time))(corner[0, 2].start)
+    pl.when(no(last_time | first_z))(corner[0, 1].start)
     shift_split(0)
     do_plane(0, 0, 3)
     do_plane(2, 0, 2)
-    down[1].wait_recv()
-    pl.when(first_time)(corner[1, 0].start)
-    shift_split(1)
-    do_plane(3, 1, 3)
-    do_plane(4, 1, 2)
-    do_plane(5, 0, 1)
-
-    def sign(d, nu):
-        return -1 if (nu, d) in PLANES else 1
-
-    for nu in range(4):
-        for c in range(8):
-            value = store[nu * 8 + c]
-            for d in others(nu):
-                moved_leaf = leaves[slot(d, nu) * 8 + c]
-                first = position(d) == 0
-                if d == 3:
-                    around = pltpu.roll(moved_leaf, LANES - NX + 1, axis=1)
-                    moved_leaf = jnp.where(first, around, pltpu.roll(moved_leaf, 1, axis=1))
-                else:
-                    moved_leaf = jnp.where(first, 0.0, turn(moved_leaf, d, 1))
-                value = value + moved_leaf if sign(d, nu) > 0 else value - moved_leaf
-            store[nu * 8 + c] = value
-
-    for d in (2, 1, 0):
+
+    def planes_z():
+        down[1].wait_recv()
+        shift_split(1)
+        do_plane(3, 1, 3)
+        do_plane(4, 1, 2)
+        do_plane(5, 0, 1)
+
+    def face(d):
         up[d].wait_recv()
         for pair in EDGES:
             if pair[0] == d:
@@ -466,16 +448,52 @@
             for c in range(8):
                 store[nu * 8 + c] += jnp.where(first, turn(faceleaf[c], d, -order), 0.0)
 
+    second_stage()
+    stages = (planes_z, functools.partial(face, 2), functools.partial(face, 0), functools.partial(face, 1))
+    orders = (
+        (no(first_time | last_z), (0, 1, 2, 3)),
+        (first_time & no(last_z), (0, 1, 3, 2)),
+        (last_z & no(first_time), (3, 2, 1, 0)),
+        (first_time & last_z, (3, 1, 0, 2)),
+    )
+
+    def take(step, carry):
+        for number, stage in enumerate(stages):
+            now = None
+            for here, order in orders:
+                hit = here & (step == order.index(number))
+                now = hit if now is None else now | hit
+            pl.when(now)(stage)
+        return carry
+
+    lax.fori_loop(0, len(stages), take, 0)
+
+    def sign(d, nu):
+        return -1 if (nu, d) in PLANES else 1
+
+    def final(nu, c):
+        value = store[nu * 8 + c]
+        for d in others(nu):
+            moved_leaf = leaves[slot(d, nu) * 8 + c]
+            first = position(d) == 0
+            if d == 3:
+                around = pltpu.roll(moved_leaf, LANES - NX + 1, axis=1)
+                moved_leaf = jnp.where(first, around, pltpu.roll(moved_leaf, 1, axis=1))
+            else:
+                moved_leaf = jnp.where(first, 0.0, turn(moved_leaf, d, 1))
+            value = value + moved_leaf if sign(d, nu) > 0 else value - moved_leaf
+        return value
+
     for mu in range(4):
         for number, (i, j) in enumerate(OFF):
-            real = store[mu * 8 + number * 2] * (0.5 * COEFF)
-            imag = store[mu * 8 + number * 2 + 1] * (0.5 * COEFF)
+            real = final(mu, number * 2) * (0.5 * COEFF)
+            imag = final(mu, number * 2 + 1) * (0.5 * COEFF)
             out_ref[comp(mu, 0, i, j)] = real
             out_ref[comp(mu, 0, j, i)] = -real
             out_ref[comp(mu, 1, i, j)] = imag
             out_ref[comp(mu, 1, j, i)] = imag
-        diag0 = store[mu * 8 + 6] * COEFF
-        diag1 = store[mu * 8 + 7] * COEFF
+        diag0 = final(mu, 6) * COEFF
+        diag1 = final(mu, 7) * COEFF
         for i, value in enumerate((diag0, diag1, -(diag0 + diag1))):
             out_ref[comp(mu, 1, i, i)] = value
             out_ref[comp(mu, 0, i, i)] = jnp.zeros_like(value)

time: 16.8 us -> 14.8 us (0.88)
  the two profiles are of different devices: /device:TPU:1 before, /device:TPU:134 now
where the time goes in v4:
time: 14.8 us; the launch traced here: 14.7 us
  Pallas kernels  13.8 us (93%)
  local copies, waits for them, and re-layouts  0.82 us (6%)
    pallas_call x1, Pallas kernels, per_device(): pl.pallas_call(kernel, out_shape=jax.ShapeDtypeStruct((72, ROWS, LANES),...  13.8 us
    unnamed x1, local copies, waits for them, and re-layouts  0.82 us

profile of v4, /device:TPU:134, one launch (start us, length us, event | category | flops | bytes accessed | tf_op | source)
XLA Modules:
  0.0 14.7 jit_solution(16526462023405119607)
XLA Ops:
  0.0 13.8 %shard_map.17 = f32[72,16,128]{2,1,0:T(8,128)S(1)} custom-call(f32[72,16,128]{2,1,0:T(8,128)} %bitcast.3), custom_call_target="tpu_custom_call" | custom-call | tf_op jit(solution)/shard_map/pallas_call | solution.py:517
  13.9 0.8 %copy.3 = f32[4,2,3,3,4,4,128]{6,5,4,3,2,1,0:T(4,128)} copy(f32[4,2,3,3,4,4,128]{6,5,4,3,2,1,0:T(4,128)S(1)} %bitcast.2) | data formatting | bytes 1179648

commit v5 on v4

--- a/solution.py
+++ b/solution.py
@@ -150,8 +150,8 @@
 TWO_ROWS = [(part, i, j) for part in range(2) for i in range(2) for j in range(3)]
 
 
-def kernel(links_ref, out_ref, u, shifted, store, leaves, wmat, send1, recv1, send2, recv2, sende, recve,
-           near, far, base, moved, faceleaf, in_sem, s1, r1, s2, r2, se, re):
+def kernel(links_ref, store, leaves, u, shifted, wmat, send1, recv1, send2, recv2, sende, recve,
+           near, far, base, moved, faceleaf, in_sem, s1, r1, s2, r2, se, re, sz, rz, ready):
     index = [lax.axis_index(name) for name in RING]
     size = [lax.axis_size(name) for name in RING]
     first_time = index[0] == 0
@@ -219,13 +219,21 @@
     pl.when(last_time)(lambda: greet(DOWN[0]))
     pl.when(last_z)(lambda: greet(DOWN[1]))
 
+    @pl.when(no(first_time))
+    def _():
+        pl.semaphore_signal(ready, inc=1, device_id=device(DOWN[0]), device_id_type=MESH)
+
     def remote(src, dst, send, recv, offset):
         return pltpu.make_async_remote_copy(
             src_ref=src, dst_ref=dst, send_sem=send, recv_sem=recv,
             device_id=device(offset), device_id_type=MESH,
         )
 
-    down = [remote(send1[d], recv1[d], s1.at[d], r1.at[d], DOWN[d]) for d in range(3)]
+    down = {d: remote(send1[d], recv1[d], s1.at[d], r1.at[d], DOWN[d]) for d in (0, 2)}
+    parts_z = [
+        remote(send1[1].at[pl.ds(3 * k, 3)], recv1[1].at[pl.ds(3 * k, 3)], sz.at[k], rz.at[k], DOWN[1])
+        for k in range(3)
+    ]
     up = [remote(send2[d], recv2[d], s2.at[d], r2.at[d], UP[d]) for d in range(3)]
     corner = {
         pair: remote(sende[n], recve[n], se.at[n], re.at[n], CORNER[n]) for n, pair in enumerate(EDGES)
@@ -244,7 +252,7 @@
     up[0].start()
     pl.when(no(first_time))(down[0].start)
     up[1].start()
-    pl.when(no(first_z))(down[1].start)
+    pl.when(no(first_z))(start(*parts_z[::-1]))
     up[2].start()
 
     def second_stage():
@@ -253,7 +261,7 @@
         pl.when(no(first_time) & first_z)(lambda: pl.semaphore_wait(barrier, 1))
         pl.when(first_z)(corner[2, 1].start)
         pl.when(first_z & no(last_time))(corner[0, 1].start)
-        pl.when(first_z)(down[1].start)
+        pl.when(first_z)(start(*parts_z[::-1]))
         pl.when(first_time)(start(corner[1, 0], corner[2, 0], down[0]))
 
     def make_w(plane, mu, nu):
@@ -281,9 +289,11 @@
             for c in range(18):
                 shifted[at + c] = shift_within_x(u[nu * 18 + c])
 
-    def shift_split(d):
+    def shift_split(d, only=None):
         edge = position(d) == COUNT[d] - 1
         for order, nu in enumerate(others(d)):
+            if only is not None and nu != only:
+                continue
             at = slot(d, nu) * 18
             got = {}
             for number, (part, i, j) in enumerate(TWO_ROWS):
@@ -419,23 +429,26 @@
         make_w(plane, mu, nu)
     for d in FACES:
         face_near(d)
+    @pl.when(no(last_time))
+    def _():
+        pl.semaphore_wait(ready, 1)
+        corner[0, 2].start()
+        pl.when(no(first_z))(corner[0, 1].start)
+
     down[2].wait_recv()
     pl.when(no(first_z))(corner[2, 1].start)
     shift_split(2)
     do_plane(1, 2, 3)
     down[0].wait_recv()
-    pl.when(no(last_time))(corner[0, 2].start)
-    pl.when(no(last_time | first_z))(corner[0, 1].start)
     shift_split(0)
     do_plane(0, 0, 3)
     do_plane(2, 0, 2)
 
     def planes_z():
-        down[1].wait_recv()
-        shift_split(1)
-        do_plane(3, 1, 3)
-        do_plane(4, 1, 2)
-        do_plane(5, 0, 1)
+        for plane, nu in ((3, 3), (4, 2), (5, 0)):
+            parts_z[others(1).index(nu)].wait_recv()
+            shift_split(1, nu)
+            do_plane(plane, *PLANES[plane])
 
     def face(d):
         up[d].wait_recv()
@@ -468,6 +481,11 @@
 
     lax.fori_loop(0, len(stages), take, 0)
 
+    for copy in list(down.values()) + parts_z + up + list(corner.values()):
+        copy.wait_send()
+
+
+def finish(store, leaves, out_ref, out, sem):
     def sign(d, nu):
         return -1 if (nu, d) in PLANES else 1
 
@@ -484,22 +502,25 @@
             value = value + moved_leaf if sign(d, nu) > 0 else value - moved_leaf
         return value
 
+    copies = []
     for mu in range(4):
         for number, (i, j) in enumerate(OFF):
             real = final(mu, number * 2) * (0.5 * COEFF)
             imag = final(mu, number * 2 + 1) * (0.5 * COEFF)
-            out_ref[comp(mu, 0, i, j)] = real
-            out_ref[comp(mu, 0, j, i)] = -real
-            out_ref[comp(mu, 1, i, j)] = imag
-            out_ref[comp(mu, 1, j, i)] = imag
+            out[comp(mu, 0, i, j)] = real
+            out[comp(mu, 0, j, i)] = -real
+            out[comp(mu, 1, i, j)] = imag
+            out[comp(mu, 1, j, i)] = imag
         diag0 = final(mu, 6) * COEFF
         diag1 = final(mu, 7) * COEFF
         for i, value in enumerate((diag0, diag1, -(diag0 + diag1))):
-            out_ref[comp(mu, 1, i, i)] = value
-            out_ref[comp(mu, 0, i, i)] = jnp.zeros_like(value)
-
-    for copy in down + up + list(corner.values()):
-        copy.wait_send()
+            out[comp(mu, 1, i, i)] = value
+            out[comp(mu, 0, i, i)] = jnp.zeros_like(value)
+        part = pl.ds(mu * 18, 18)
+        copies.append(pltpu.make_async_copy(out.at[part], out_ref.at[part], sem.at[mu]))
+        copies[-1].start()
+    for copy in copies:
+        copy.wait()
 
 
 def per_device(links):
@@ -512,21 +533,29 @@
     counts1 = [-(-36 // g) for g in GROUP]
     counts2 = (12, 12, 6)
     edges = [vmem((ROWS, LANES), jnp.float32) for _ in EDGES]
-    arrays = (72, 216, 32, 96, 108)
+    arrays = (72, 216, 108)
     dma = pltpu.SemaphoreType.DMA
-    out = pl.pallas_call(
+    store, leaves = pl.pallas_call(
         kernel,
-        out_shape=jax.ShapeDtypeStruct((72, ROWS, LANES), jnp.float32),
+        out_shape=[jax.ShapeDtypeStruct((n, ROWS, LANES), jnp.float32) for n in (32, 96)],
         in_specs=[pl.BlockSpec(memory_space=pltpu.HBM)],
-        out_specs=pl.BlockSpec(memory_space=pltpu.VMEM),
+        out_specs=[pl.BlockSpec(memory_space=pltpu.VMEM)] * 2,
         scratch_shapes=packed(arrays)
         + [packed(counts1), packed(counts1), packed(counts2), packed(counts2), edges, edges]
         + packed((54, 18, 18, 18, 8))
-        + [dma((n,)) for n in (4, 3, 3, 3, 3, 6, 6)],
+        + [dma((n,)) for n in (4, 3, 3, 3, 3, 6, 6, 3, 3)] + [pltpu.SemaphoreType.REGULAR],
         compiler_params=pltpu.CompilerParams(
             collective_id=0, has_side_effects=True, vmem_limit_bytes=16 * 1024 * 1024
         ),
     )(pltpu.with_memory_space_constraint(links.reshape(72, ROWS, LANES), pltpu.HBM))
+    out = pl.pallas_call(
+        finish,
+        out_shape=jax.ShapeDtypeStruct((72, ROWS, LANES), jnp.float32),
+        in_specs=[pl.BlockSpec(memory_space=pltpu.VMEM)] * 2,
+        out_specs=pl.BlockSpec(memory_space=pltpu.HBM),
+        scratch_shapes=[vmem((72, ROWS, LANES), jnp.float32), dma((4,))],
+        compiler_params=pltpu.CompilerParams(vmem_limit_bytes=16 * 1024 * 1024),
+    )(store, leaves)
     return out.reshape(shape)
 
 

time: 14.8 us -> 14.5 us (0.980)
  the two profiles are of different devices: /device:TPU:134 before, /device:TPU:6 now
where the time goes in v5:
time: 14.5 us; the launch traced here: 14.3 us
  Pallas kernels  14.3 us (99%)
    pallas_call x1, Pallas kernels, per_device(): pl.pallas_call(kernel, out_shape=[jax.ShapeDtypeStruct((n, ROWS, LANES),...  13.3 us
    pallas_call x1, Pallas kernels, per_device(): pl.pallas_call(finish, out_shape=jax.ShapeDtypeStruct((72, ROWS, LANES),...  0.97 us

profile of v5, /device:TPU:6, one launch (start us, length us, event | category | flops | bytes accessed | tf_op | source)
XLA Modules:
  0.0 14.3 jit_solution(5692608405564036004)
XLA Ops:
  0.0 13.3 %shard_map.17 = (f32[32,16,128]{2,1,0:T(8,128)S(1)}, f32[96,16,128]{2,1,0:T(8,128)S(1)}) custom-call(f32[72,16,128]{2,1,0:T(8,128)} %bitcast.2), custom_call_target="tpu_custom_call" | custom-call | tf_op jit(solution)/shard_map/pallas_call | solution.py:538
  13.3 1.0 %shard_map.18 = f32[72,16,128]{2,1,0:T(8,128)} custom-call(f32[32,16,128]{2,1,0:T(8,128)S(1)} %get-tuple-element.7.store, f32[96,16,128]{2,1,0:T(8,128)S(1)} %get-tuple-element.8.leaves), custom_call_target="tpu_custom_call" | custom-call | tf_op jit(solution)/shard_map/pallas_call | solution.py:551
